TPU v7x, 16 devices: a 4x2x1 block of a 4x4x8 slice. The times are simulated.
16 devices in a mesh: dp: 2 (over y, z), cp: 8 (over x, core).
Axes of the slice: x: 4, y: 2, z: 1, core: 2. Of those that a mesh axis runs over, the one named last changes fastest.
The devices are a block of a 4x4x8 slice.
Arguments:
- x_in: bfloat16 [4096, 1536], P(('dp', 'cp')), parts along dimension 0
- d_y: bfloat16 [4096, 1536], P(('dp', 'cp')), parts along dimension 0
- w_q: bfloat16 [1536, 12, 128], replicated
- w_k: bfloat16 [1536, 2, 128], replicated
- w_v: bfloat16 [1536, 2, 128], replicated
- w_o: bfloat16 [12, 128, 1536], replicated
Outputs:
- output: bfloat16 [4096, 1536], P(('dp', 'cp')), parts along dimension 0
There are 2 independent parts. A program takes and returns all parts, laid end to end along the dimension named above; an argument that names none is the same for every part.
All inputs are finite; a program needn't handle non-finite values.
Results may differ from a plain program's by a relative error of at most 0.0113783.
Values are sent between devices in bfloat16 or wider.
A program may use at most 768 MiB of HBM per device.

v0:
```python
import math
import jax
import jax.numpy as jnp
from jax import lax
from jax.sharding import PartitionSpec as P


def block_rows(row_total, key_total, head_total):
    budget = max(1, 2 ** 23 // (key_total * head_total))
    return math.gcd(row_total, max(8, 2 ** int(math.log2(budget))))


def token_positions(row_ids, tok_len, n_dev):
    dev_idx = row_ids // tok_len
    row_off = row_ids % tok_len
    seg_len = tok_len // 2
    seg_idx = jnp.where(row_off < seg_len, dev_idx, 2 * n_dev - 1 - dev_idx)
    return seg_idx * seg_len + row_off % seg_len


def solution(mesh):
    n_dev = mesh.shape["cp"]
    row_spec = P(("dp", "cp"), None)

    def device_fn(x_in, d_y, w_q, w_k, w_v, w_o):
        tok_len, d_model = x_in.shape
        q_heads, head_dim = w_q.shape[1], w_q.shape[2]
        kv_heads = w_k.shape[1]
        q_group = q_heads // kv_heads
        seq_len = tok_len * n_dev
        score_scale = head_dim ** -0.5
        dev_rank = lax.axis_index("cp")
        wq_grp = w_q.reshape(d_model, kv_heads, q_group, head_dim)
        wo_grp = w_o.reshape(kv_heads, q_group, head_dim, d_model)
        q_loc = jnp.einsum("td,dkge->tkge", x_in, wq_grp, preferred_element_type=jnp.float32).astype(jnp.bfloat16)
        k_loc = jnp.einsum("td,dke->tke", x_in, w_k, preferred_element_type=jnp.float32).astype(jnp.bfloat16)
        v_loc = jnp.einsum("td,dke->tke", x_in, w_v, preferred_element_type=jnp.float32).astype(jnp.bfloat16)
        do_loc = jnp.einsum("td,kged->tkge", d_y, wo_grp, preferred_element_type=jnp.float32).astype(jnp.bfloat16)
        k_all = lax.all_gather(k_loc, "cp", axis=0, tiled=True)
        v_all = lax.all_gather(v_loc, "cp", axis=0, tiled=True)
        pos_all = token_positions(jnp.arange(seq_len), tok_len, n_dev)
        pos_loc = token_positions(dev_rank * tok_len + jnp.arange(tok_len), tok_len, n_dev)
        blk_rows = block_rows(tok_len, seq_len, q_heads)

        def block_step(acc_pair, blk_idx):
            dk_acc, dv_acc = acc_pair
            row_start = blk_idx * blk_rows
            q_blk = lax.dynamic_slice_in_dim(q_loc, row_start, blk_rows, 0)
            do_blk = lax.dynamic_slice_in_dim(do_loc, row_start, blk_rows, 0)
            pos_blk = lax.dynamic_slice_in_dim(pos_loc, row_start, blk_rows, 0)
            scores = jnp.einsum("rkge,ske->krgs", q_blk, k_all, preferred_element_type=jnp.float32) * score_scale
            causal = pos_blk[None, :, None, None] >= pos_all[None, None, None, :]
            scores = jnp.where(causal, scores, -jnp.inf)
            lse_blk = jax.nn.logsumexp(scores, axis=-1, keepdims=True)
            prob_blk = jnp.exp(scores - lse_blk).astype(jnp.bfloat16)
            out_blk = jnp.einsum("krgs,ske->krge", prob_blk, v_all, preferred_element_type=jnp.float32).astype(jnp.bfloat16)
            row_delta = jnp.einsum("rkge,krge->krg", do_blk, out_blk, preferred_element_type=jnp.float32)
            dp_blk = jnp.einsum("rkge,ske->krgs", do_blk, v_all, preferred_element_type=jnp.float32)
            ds_blk = (prob_blk * (dp_blk - row_delta[..., None])).astype(jnp.bfloat16)
            dq_blk = (jnp.einsum("krgs,ske->krge", ds_blk, k_all, preferred_element_type=jnp.float32) * score_scale).astype(jnp.bfloat16)
            dk_acc = dk_acc + jnp.einsum("krgs,rkge->kse", ds_blk, q_blk, preferred_element_type=jnp.float32)
            dv_acc = dv_acc + jnp.einsum("krgs,rkge->kse", prob_blk, do_blk, preferred_element_type=jnp.float32)
            return (dk_acc, dv_acc), dq_blk

        zero_acc = jnp.zeros((kv_heads, seq_len, head_dim), jnp.float32)
        (dk_part, dv_part), dq_blocks = lax.scan(block_step, (zero_acc, zero_acc), jnp.arange(tok_len // blk_rows))
        d_key = lax.psum_scatter(dk_part * score_scale, "cp", scatter_dimension=1, tiled=True).astype(jnp.bfloat16)
        d_value = lax.psum_scatter(dv_part, "cp", scatter_dimension=1, tiled=True).astype(jnp.bfloat16)
        d_x = jnp.einsum("bkrge,dkge->brd", dq_blocks, wq_grp, preferred_element_type=jnp.float32).reshape(tok_len, d_model)
        d_x = d_x + jnp.einsum("kte,dke->td", d_key, w_k, preferred_element_type=jnp.float32)
        d_x = d_x + jnp.einsum("kte,dke->td", d_value, w_v, preferred_element_type=jnp.float32)
        return d_x.astype(jnp.bfloat16)

    return jax.shard_map(device_fn, mesh=mesh, in_specs=(row_spec, row_spec, P(), P(), P(), P()), out_specs=row_spec, check_vma=False)
```

profile of v0, /device:TPU:112, one launch (start us, length us, event | category | flops | bytes accessed | tf_op | source)
XLA Modules:
  0.0 164.2 jit_solution(627598836270908158)
XLA Ops:
  6.5 0.0 copy-start
  6.6 0.0 all-gather.3.cloned.1.call-start
  6.6 2.5 %convolution_convert_fusion.3 = bf16[256,2,128]{2,0,1:T(8,128)(2,1)} fusion(bf16[256,1536]{1,0:T(8,128)(2,1)} %param.6, bf16[1536,2,128]{2,1,0:T(2,128)(2,1)} %param.9), kind=kOutput, calls=%fused_computation.24 | convolution fusion | flops 201392128 | bytes 1703936 | tf_op jit(solution)/shard_map/td,dke->tke/dot_general | solution.py:36
  9.0 0.1 all-gather.3.cloned.1.call-update
  9.1 0.1 all-gather.5.cloned.1.call-start
  9.2 2.4 %convolution_convert_fusion.2 = bf16[256,2,128]{2,0,1:T(8,128)(2,1)} fusion(bf16[256,1536]{1,0:T(8,128)(2,1)} %param.6, bf16[1536,2,128]{2,1,0:T(2,128)(2,1)} %param.10), kind=kOutput, calls=%fused_computation.23 | convolution fusion | flops 201392128 | bytes 1703936 | tf_op jit(solution)/shard_map/td,dke->tke/dot_general | solution.py:37
  11.6 0.1 all-gather.5.cloned.1.call-update
  11.6 0.1 reduce-scatter.3.cloned.1.call-start
  11.7 4.0 %convolution_convert_fusion.1 = bf16[256,2,6,128]{3,0,2,1:T(8,128)(2,1)S(1)} fusion(bf16[1536,2,6,128]{3,0,2,1:T(8,128)(2,1)} %bitcast.71, bf16[256,1536]{1,0:T(8,128)(2,1)} %param.6), kind=kOutput, calls=%fused_computation.22 | convolution fusion | flops 1208352768 | bytes 6291456 | tf_op jit(solution)/shard_map/td,dkge->tkge/dot_general | solution.py:35
  15.7 0.4 broadcast_compare_fusion
  16.1 0.0 copy-done
  16.1 5.0 %bitcast_convert_fusion = (f32[2,256,6,128]{3,1,2,0:T(8,128)}, bf16[256,2,6,128]{3,0,2,1:T(8,128)(2,1)S(1)}) fusion(bf16[2,6,128,1536]{3,2,1,0:T(8,128)(2,1)} %bitcast.70, bf16[256,1536]{1,0:T(8,128)(2,1)S(1)} %copy-done), kind=kOutput, calls=%fused_computation.36 | convolution fusion | flops 1208745984 | bytes 7864320 | tf_op jit(solution)/shard_map/td,kged->tkge/dot_general | solution.py:38
  21.1 10.0 %all-gather.3.cloned.1.call-done = bf16[2048,2,128]{2,0,1:T(8,128)(2,1)} async-done(((bf16[256,2,128]{2,0,1:T(8,128)(2,1)}), bf16[2048,2,128]{2,0,1:T(8,128)(2,1)}) %all-gather.3.cloned.1.call-update) | async-done | bytes 1048592 | tf_op jit(solution)/shard_map/all_gather | solution.py:39
  31.1 11.6 %fusion = (f32[2,256,6]{1,2,0:T(8,128)S(1)}, f32[2,256,6,2048]{3,1,2,0:T(8,128)}) fusion(pred[256,2048]{1,0:T(8,128)(4,1)S(1)} %broadcast_compare_fusion, bf16[256,2,6,128]{3,0,2,1:T(8,128)(2,1)S(1)} %convolution_convert_fusion.1, bf16[2048,2,128]{2,0,1:T(8,128)(2,1)} %all-gather.3.cloned.1.call-done), kind=kOutput, calls=%fused_computation.4 | convolution fusion | flops 1629484032 | bytes 27537408 | tf_op jit(solution)/shard_map/while/body/eval_jaxpr/rkge,ske->krgs/dot_general | solution.py:51
  42.7 12.0 %exponential_reduce_fusion = f32[2,256,6]{1,2,0:T(8,128)S(1)} fusion(f32[2,256,6,2048]{3,1,2,0:T(8,128)} %get-tuple-element.24, f32[2,256,6]{1,2,0:T(8,128)S(1)} %is-finite_select_fusion, pred[256,2048]{1,0:T(8,128)(4,1)S(1)} %broadcast_compare_fusion), kind=kLoop, calls=%fused_computation.2 | loop fusion | flops 25162752 | bytes 25714688 | tf_op jit(solution)/shard_map/while/body/eval_jaxpr/reduce_sum | solution.py:54
  54.8 3.4 %copy-done.2 = f32[2,256,6,2048]{3,1,2,0:T(8,128)S(1)} copy-done((f32[2,256,6,2048]{3,1,2,0:T(8,128)S(1)}, f32[2,256,6,2048]{3,1,2,0:T(8,128)}, u32[]{:S(2)}) %copy-start.2) | copy-done | bytes 25165848
  58.1 7.4 %exponential_convert_fusion = bf16[2,256,6,2048]{3,1,2,0:T(8,128)(2,1)} fusion(f32[2,256,6,2048]{3,1,2,0:T(8,128)S(1)} %copy-done.2, f32[2,256,6]{1,2,0:T(8,128)S(1)} %log_add_fusion, pred[256,2048]{1,0:T(8,128)(4,1)S(1)} %broadcast_compare_fusion), kind=kLoop, calls=%fused_computation.1 | loop fusion | flops 25165824 | bytes 38285312 | tf_op jit(solution)/shard_map/while/body/eval_jaxpr/convert_element_type | solution.py:55
  65.5 8.4 %fusion.18 = bf16[2,256,6,128]{3,1,2,0:T(8,128)(2,1)S(1)} fusion(bf16[2,256,6,2048]{3,1,2,0:T(8,128)(2,1)} %exponential_convert_fusion, bf16[2048,2,128]{2,0,1:T(8,128)(2,1)} %all-gather.5.cloned.1.call-done), kind=kOutput, calls=%fused_computation.27 | convolution fusion | flops 1610612736 | bytes 14417920 | tf_op jit(solution)/shard_map/while/body/eval_jaxpr/krgs,ske->krge/dot_general | solution.py:56
  73.9 1.5 multiply_reduce_fusion
  75.4 0.1 copy.22
  75.5 9.1 %multiply_convert_fusion = bf16[2,256,6,2048]{3,1,2,0:T(8,128)(2,1)} fusion(bf16[2,256,6,2048]{3,1,2,0:T(8,128)(2,1)} %exponential_convert_fusion, f32[2,256,6]{1,2,0:T(8,128)S(1)} %copy.22, bf16[256,2,6,128]{3,0,2,1:T(8,128)(2,1)S(1)} %get-tuple-element.26, bf16[2048,2,128]{2,0,1:T(8,128)(2,1)S(1)} %copy-done.5), kind=kOutput, calls=%fused_computation | convolution fusion | flops 1635778560 | bytes 27013120 | tf_op jit(solution)/shard_map/while/body/eval_jaxpr/rkge,ske->krgs/dot_general | solution.py:58
  84.6 9.4 %fusion.11 = f32[2,2048,128]{2,1,0:T(8,128)} fusion(bf16[2,256,6,2048]{3,1,2,0:T(8,128)(2,1)} %multiply_convert_fusion, bf16[256,2,6,128]{3,0,2,1:T(8,128)(2,1)S(1)} %convolution_convert_fusion.1), kind=kOutput, calls=%fused_computation.15 | convolution fusion | flops 1611137024 | bytes 15466496 | tf_op jit(solution)/shard_map/while/body/eval_jaxpr/krgs,rkge->kse/dot_general | solution.py:61
  94.0 0.1 reduce-scatter.3.cloned.1.call-update
  94.1 0.1 reduce-scatter.5.cloned.1.call-start
  94.2 9.4 %convolution_bitcast_fusion.1 = f32[2,2048,128]{2,1,0:T(8,128)} fusion(bf16[2,256,6,2048]{3,1,2,0:T(8,128)(2,1)} %exponential_convert_fusion, bf16[256,2,6,128]{3,0,2,1:T(8,128)(2,1)S(1)} %get-tuple-element.26), kind=kOutput, calls=%fused_computation.12 | convolution fusion | flops 1610612736 | bytes 15466496 | tf_op jit(solution)/shard_map/while/body/eval_jaxpr/krgs,rkge->kse/dot_general | solution.py:62
  103.6 0.1 reduce-scatter.5.cloned.1.call-update
  103.6 20.3 %reduce-scatter.3.cloned.1.call-done = f32[2,256,128]{2,1,0:T(8,128)} async-done(((f32[2,2048,128]{2,1,0:T(8,128)}), f32[2,256,128]{2,1,0:T(8,128)}) %reduce-scatter.3.cloned.1.call-update) | async-done | bytes 262160 | tf_op jit(solution)/shard_map/reduce_scatter | solution.py:67
  123.9 1.7 %convolution_bitcast_fusion.2 = f32[256,1536]{1,0:T(8,128)S(1)} fusion(bf16[1536,2,128]{2,1,0:T(2,128)(2,1)} %param.9, f32[2,256,128]{2,1,0:T(8,128)} %reduce-scatter.3.cloned.1.call-done), kind=kOutput, calls=%fused_computation.13 | convolution fusion | flops 201392128 | bytes 2621440 | tf_op jit(solution)/shard_map/kte,dke->td/dot_general | solution.py:70
  125.6 11.8 %fusion.8 = f32[256,1536]{1,0:T(8,128)} fusion(f32[256,1536]{1,0:T(8,128)S(1)} %convolution_bitcast_fusion.2, bf16[1536,2,6,128]{3,0,2,1:T(8,128)(2,1)} %bitcast.72, bf16[2,256,6,2048]{3,1,2,0:T(8,128)(2,1)} %multiply_convert_fusion, bf16[2048,2,128]{2,0,1:T(8,128)(2,1)S(1)} %copy-done.4), kind=kOutput, calls=%fused_computation.10 | convolution fusion | flops 2819751936 | bytes 21495808 | tf_op jit(solution)/shard_map/bkrge,dkge->brd/dot_general | solution.py:69
  137.4 17.2 %reduce-scatter.5.cloned.1.call-done = f32[2,256,128]{2,1,0:T(8,128)} async-done(((f32[2,2048,128]{2,1,0:T(8,128)}), f32[2,256,128]{2,1,0:T(8,128)}) %reduce-scatter.5.cloned.1.call-update) | async-done | bytes 262160 | tf_op jit(solution)/shard_map/reduce_scatter | solution.py:68
  154.6 3.0 %fusion.13 = bf16[256,1536]{1,0:T(8,128)(2,1)} fusion(f32[256,1536]{1,0:T(8,128)} %fusion.8, bf16[1536,2,128]{2,1,0:T(2,128)(2,1)} %param.10, f32[2,256,128]{2,1,0:T(8,128)} %reduce-scatter.5.cloned.1.call-done), kind=kOutput, calls=%fused_computation.17 | convolution fusion | flops 202178560 | bytes 3407872 | tf_op jit(solution)/shard_map/kte,dke->td/dot_general | solution.py:71
  157.6 0.0 copy-done.1
  (13 shorter events, 0.1 us)
Async XLA Ops:
  6.5 9.5 %copy-start = (bf16[256,1536]{1,0:T(8,128)(2,1)S(1)}, bf16[256,1536]{1,0:T(8,128)(2,1)}, u32[]{:S(2)}) copy-start(bf16[256,1536]{1,0:T(8,128)(2,1)} %param.7) | copy-start | bytes 2359300
  6.6 24.6 %all-gather.3.cloned.1.call-start = ((), (), s32[]{:S(2)}) async-start(), calls=%async_computation.2 | async-start | bytes 1179648 | tf_op jit(solution)/shard_map/all_gather | solution.py:39
  9.1 56.4 %all-gather.5.cloned.1.call-start = ((), (), s32[]{:S(2)}) async-start(), calls=%async_computation.3 | async-start | bytes 1179648 | tf_op jit(solution)/shard_map/all_gather | solution.py:40
  11.6 112.3 %reduce-scatter.3.cloned.1.call-start = ((), (), s32[]{:S(2)}) async-start(), calls=%async_computation.4 | async-start | bytes 2359296 | tf_op jit(solution)/shard_map/reduce_scatter | solution.py:67
  42.7 15.4 %copy-start.2 = (f32[2,256,6,2048]{3,1,2,0:T(8,128)S(1)}, f32[2,256,6,2048]{3,1,2,0:T(8,128)}, u32[]{:S(2)}) copy-start(f32[2,256,6,2048]{3,1,2,0:T(8,128)} %get-tuple-element.24) | copy-start | bytes 75497472
  65.5 8.4 %copy-start.3 = (f32[2,256,6,128]{3,1,2,0:T(8,128)S(1)}, f32[2,256,6,128]{3,1,2,0:T(8,128)}, u32[]{:S(2)}) copy-start(f32[2,256,6,128]{3,1,2,0:T(8,128)} %get-tuple-element.25) | copy-start | bytes 4718596
  65.5 10.0 %copy-start.5 = (bf16[2048,2,128]{2,0,1:T(8,128)(2,1)S(1)}, bf16[2048,2,128]{2,0,1:T(8,128)(2,1)}, u32[]{:S(2)}) copy-start(bf16[2048,2,128]{2,0,1:T(8,128)(2,1)} %all-gather.5.cloned.1.call-done) | copy-start | bytes 3145732
  94.0 31.5 %copy-start.4 = (bf16[2048,2,128]{2,0,1:T(8,128)(2,1)S(1)}, bf16[2048,2,128]{2,0,1:T(8,128)(2,1)}, u32[]{:S(2)}) copy-start(bf16[2048,2,128]{2,0,1:T(8,128)(2,1)} %all-gather.3.cloned.1.call-done) | copy-start | bytes 3145732
  94.1 60.5 %reduce-scatter.5.cloned.1.call-start = ((), (), s32[]{:S(2)}) async-start(), calls=%async_computation.5 | async-start | bytes 2359296 | tf_op jit(solution)/shard_map/reduce_scatter | solution.py:68
  123.9 33.8 %copy-start.1 = (bf16[256,1536]{1,0:T(8,128)(2,1)S(1)}, bf16[256,1536]{1,0:T(8,128)(2,1)}, u32[]{:S(2)}) copy-start(bf16[256,1536]{1,0:T(8,128)(2,1)} %param.7) | copy-start | bytes 2359300
Sparse Core Ops, SparseCore 0:
  9.2 21.8 all-gather.2
  32.7 18.8 all-gather.4
  94.2 29.6 reduce-scatter.2
  126.0 28.5 reduce-scatter.4
where the time goes:
time: 164 us
  matrix products  78.2 us (48%)
  waiting for transfers between devices  47.8 us (29%)
  other arithmetic  21.2 us (13%)
  between operations  13.2 us (8%)
  local copies, waits for them, and re-layouts  3.49 us (2%)
    reduce_scatter x1, waiting for transfers between devices, device_fn(): lax.psum_scatter(dk_part * score_scale, 'cp', scatter_dimension=1, tiled=...  20.3 us
    reduce_scatter x1, waiting for transfers between devices, device_fn(): lax.psum_scatter(dv_part, 'cp', scatter_dimension=1, tiled=True)  17.2 us
    reduce_sum x1, other arithmetic, block_step(): lse_blk = jax.nn.logsumexp(scores, axis=-1, keepdims=True)  12 us
    dot_general x1, matrix products, device_fn(): jnp.einsum('bkrge,dkge->brd', dq_blocks, wq_grp, preferred_element_type=j...  11.8 us
    dot_general x1, matrix products, block_step(): jnp.einsum('rkge,ske->krgs', q_blk, k_all, preferred_element_type=jnp.flo...  11.6 us
    all_gather x1, waiting for transfers between devices, device_fn(): k_all = lax.all_gather(k_loc, 'cp', axis=0, tiled=True)  10 us
    dot_general x1, matrix products, block_step(): jnp.einsum('krgs,rkge->kse', ds_blk, q_blk, preferred_element_type=jnp.fl...  9.4 us
    dot_general x1, matrix products, block_step(): jnp.einsum('krgs,rkge->kse', prob_blk, do_blk, preferred_element_type=jnp...  9.37 us
  transfers between devices with their start and end apart: 4, of which 3 were waited for; matrix products, arithmetic and copies ran while one was open for 40% of the time, Pallas kernels for 0%

commit v1 on v0

v1 whole, which is shorter than its diff:
```python
import functools
import math

import jax
import jax.numpy as jnp
from jax import lax
from jax.experimental import pallas as pl
from jax.experimental.pallas import tpu as pltpu
from jax.sharding import PartitionSpec as P

MESH = pl.DeviceIdType.MESH
BF = jnp.bfloat16
F32 = jnp.float32
OWN, LF, RT, OP = 0, 1, 2, 3
NT = (((1,), (1,)), ((), ()))


def dot(a, b):
    return jnp.dot(a, b, preferred_element_type=F32)


def dot_nt(a, b):
    return lax.dot_general(a, b, NT, preferred_element_type=F32)


def kernel(n_dev, x_hbm, dy_hbm, wq_hbm, wk_hbm, wv_hbm, wo_hbm, out_hbm,
           x_v, dy_v, wq_v, wk_v, wv_v, wo_v, wf_v, wkv_v,
           kv_send, kvbuf, q_send, do_send, qbuf, dobuf,
           est, dpst, m_run, l_run, d_run, m_ent, p_buf, ds_buf, dqt,
           pacc, pown, m1_lf, m1_rt, fin, fin_own, dq_send, dq_rows, acc, out_v, dkv, dq_tmp,
           ld_sem, st_sem, kvs, kvr, kvps, kvrs, qs, qr, m1s, m1r, m2s, m2r, fos, dqs, dqr):
    me = lax.axis_index("cp")
    n_chip = n_dev // 2
    c = me // 2
    h = me % 2
    ho = 1 - h
    right = lax.rem(c + 1, n_chip)
    left = lax.rem(c + n_chip - 1, n_chip)
    opp = lax.rem(c + 2, n_chip)
    rows, d_model = x_v.shape
    seg = rows // 2
    blk_len = kvbuf.shape[2]
    hd = qbuf.shape[3]
    groups = qbuf.shape[1]
    scale = hd ** -0.5
    scale2 = scale * math.log2(math.e)

    def off(blk, core):
        r = core if blk == 0 else 1 - core
        return pl.multiple_of(r * seg, seg)

    def rc(src, dst, ssem, rsem, chip, core):
        return pltpu.make_async_remote_copy(src_ref=src, dst_ref=dst, send_sem=ssem, recv_sem=rsem,
                                            device_id={"cp": chip * 2 + core}, device_id_type=MESH)

    loads = [pltpu.make_async_copy(a, b, ld_sem.at[i]) for i, (a, b) in enumerate([
        (wk_hbm, wk_v), (wv_hbm, wv_v), (x_hbm, x_v), (wq_hbm, wq_v), (dy_hbm, dy_v), (wo_hbm, wo_v)])]
    for cp in loads:
        cp.start()

    barrier = pltpu.get_barrier_semaphore()
    for chip, core in ((c, ho), (right, 0), (right, 1), (left, 0), (left, 1)):
        pl.semaphore_signal(barrier, inc=1, device_id={"cp": chip * 2 + core}, device_id_type=MESH)

    for j, (ld, w) in enumerate(((loads[0], wk_v), (loads[1], wv_v))):
        ld.wait()
        wf_v[...] = w[...].astype(F32)
        for hh in range(2):
            wkv_v[hh, :, j * hd:(j + 1) * hd] = wf_v[pl.ds(hh, d_model, stride=2), :].astype(BF)
    loads[2].wait()
    for hh in range(2):
        kv_send[hh] = dot(x_v[...], wkv_v[hh]).astype(BF)
    for blk in range(2):
        kvbuf[OWN, blk, pl.ds(off(blk, h), seg), :] = kv_send[h, blk * seg:(blk + 1) * seg, :]

    pl.semaphore_wait(barrier, 5)

    kv_sends = []
    for blk in range(2):
        kv_sends.append(rc(kv_send.at[ho, pl.ds(blk * seg, seg), :],
                           kvbuf.at[OWN, blk, pl.ds(off(blk, h), seg), :],
                           kvps.at[blk], kvr.at[OWN, h, blk], c, ho))
    dirs = []
    for first in range(2):
        go_right = (h == first)
        chip = jnp.where(go_right, right, left)
        slot = jnp.where(go_right, LF, RT)
        dirs.append([rc(kv_send.at[hh, pl.ds(blk * seg, seg), :],
                        kvbuf.at[slot, blk, pl.ds(off(blk, h), seg), :],
                        kvs.at[first, hh, blk], kvr.at[slot, h, blk], chip, hh)
                     for hh in range(2) for blk in range(2)])
    for cp in dirs[0]:
        cp.start()
    for cp in kv_sends:
        cp.start()

    def project(dst, src, grp, w_is_q):
        for p in range(groups // 2):
            if w_is_q:
                a = grp * groups + 2 * p
                w = jnp.concatenate([wq_v[a], wq_v[a + 1]], axis=1)
                r = dot(src[...], w).astype(BF)
            else:
                w = wo_v[pl.ds(pl.multiple_of((grp * groups + 2 * p) * hd, hd), 2 * hd), :]
                r = dot_nt(src[...], w).astype(BF)
            for k in range(2):
                dst(2 * p + k, r[:, k * hd:(k + 1) * hd])

    def to_send(buf):
        def put(g, val):
            buf[g] = val
        return put

    def to_own(buf):
        def put(g, val):
            for t in range(2):
                buf[t, g, pl.ds(off(t, h), seg), :] = val[t * seg:(t + 1) * seg]
        return put

    def xsends(buf, dst, k):
        return [rc(buf.at[:, pl.ds(t * seg, seg), :], dst.at[t, :, pl.ds(off(t, h), seg), :],
                   qs.at[k, t], qr.at[k, t], c, ho) for t in range(2)]

    loads[3].wait()
    project(to_send(q_send), x_v, ho, True)
    q_sends = xsends(q_send, qbuf, 0)
    for cp in q_sends:
        cp.start()
    for cp in dirs[1]:
        cp.start()
    project(to_own(qbuf), x_v, h, True)
    loads[4].wait()
    loads[5].wait()
    project(to_send(do_send), dy_v, ho, False)
    do_sends = xsends(do_send, dobuf, 1)
    for cp in do_sends:
        cp.start()

    relays = []
    for core, slot, chip in ((0, LF, right), (1, RT, left)):
        for blk in range(2):
            view = kvbuf.at[slot, blk, pl.ds(off(blk, core), seg), :]
            rc(view, view, kvs.at[0, 0, blk], kvr.at[slot, core, blk], chip, h).wait_recv()
            cp = rc(view, kvbuf.at[OP, blk, pl.ds(off(blk, core), seg), :],
                    kvrs.at[core, blk], kvr.at[OP, core, blk], chip, h)
            cp.start()
            relays.append(cp)

    project(to_own(dobuf), dy_v, h, False)

    def fwd(ent, t, slot, blk, diag, init):
        kv = kvbuf[slot, blk]
        k, v = kv[:, :hd], kv[:, hd:]
        for g in range(groups):
            s = dot_nt(k, qbuf[t, g]) * scale2
            dp = dot_nt(v, dobuf[t, g])
            if diag:
                key_pos = lax.broadcasted_iota(jnp.int32, s.shape, 0)
                q_pos = lax.broadcasted_iota(jnp.int32, s.shape, 1)
                s = jnp.where(key_pos > q_pos, -jnp.inf, s)
            m = jnp.max(s, axis=0, keepdims=True)
            if not init:
                m_old = m_run[t, g]
                m = jnp.maximum(m, m_old)
            e = jnp.exp2(s - m)
            l = jnp.sum(e, axis=0, keepdims=True)
            d = jnp.sum(e * dp, axis=0, keepdims=True)
            if not init:
                alpha = jnp.exp2(m_old - m)
                l = l_run[t, g] * alpha + l
                d = d_run[t, g] * alpha + d
            est[ent, g] = e
            dpst[ent, g] = dp
            m_ent[ent, g] = m
            m_run[t, g] = m
            l_run[t, g] = l
            d_run[t, g] = d

    def wait_kv(slot, core, blk):
        view = kvbuf.at[slot, blk, pl.ds(off(blk, core), seg), :]
        rc(view, view, kvs.at[0, 0, 0], kvr.at[slot, core, blk], left, h).wait_recv()

    for k, dst in enumerate((qbuf, dobuf)):
        for t in range(2):
            view = dst.at[t, :, pl.ds(off(t, ho), seg), :]
            rc(view, view, qs.at[k, t], qr.at[k, t], c, ho).wait_recv()
    for blk in range(2):
        wait_kv(OWN, ho, blk)
    fwd(0, 0, OWN, 0, True, True)
    fwd(1, 1, OWN, 1, True, True)
    fwd(2, 1, OWN, 0, False, False)

    def owner_of(slot):
        return jnp.where(slot == LF, left, jnp.where(slot == RT, right, opp))

    def fwd_body(i, carry):
        slot = i + 1

        @pl.when(i == 0)
        def _():
            for blk in range(2):
                wait_kv(LF, 1, blk)

        @pl.when(i == 1)
        def _():
            for blk in range(2):
                wait_kv(RT, 0, blk)

        @pl.when(i == 2)
        def _():
            for core in range(2):
                for blk in range(2):
                    wait_kv(OP, core, blk)

        later = (owner_of(slot) > c).astype(jnp.int32)
        fwd(3 + 2 * i, 1, slot, 0, False, False)
        fwd(4 + 2 * i, later, slot, later, False, False)
        return carry

    lax.fori_loop(0, 3, fwd_body, 0)

    for t in range(2):
        for g in range(groups):
            l = l_run[t, g]
            d_run[t, g] = d_run[t, g] / l
            m_run[t, g] = m_run[t, g] + jnp.log2(l)

    dqt[...] = jnp.zeros_like(dqt)

    def bwd(ent, t, slot, blk):
        for g in range(groups):
            w = jnp.exp2(m_ent[ent, g] - m_run[t, g])
            p = (est[ent, g] * w).astype(BF)
            p_buf[:, g * blk_len:(g + 1) * blk_len] = p
            ds_buf[:, g * blk_len:(g + 1) * blk_len] = (
                p.astype(F32) * (dpst[ent, g] - d_run[t, g])).astype(BF)
        kt = kvbuf[slot, blk][:, :hd].T
        dqt[t] += dot(kt, ds_buf[...])
        dk = dot(ds_buf[...], qbuf[t].reshape(groups * blk_len, hd))
        dv = dot(p_buf[...], dobuf[t].reshape(groups * blk_len, hd))
        return dk, dv

    def put(ref, pair):
        ref[:, :hd] = pair[0]
        ref[:, hd:] = pair[1]

    def add(ref, pair):
        ref[:, :hd] += pair[0]
        ref[:, hd:] += pair[1]

    def half(ref, blk, k):
        return ref.at[blk, pl.ds(k * seg, seg), :]

    def m2copy(slot, blk, k):
        chip = right if slot == RT else left
        side = 0 if slot == RT else 1
        core = k if blk == 0 else 1 - k
        return rc(half(pacc.at[slot], blk, k), fin.at[side, h, blk], m2s.at[side, blk, k],
                  m2r.at[side, h, blk], chip, core)

    m1_copies = []
    for blk in range(2):
        m1_copies.append(rc(half(pacc.at[OP], blk, 0), m1_lf.at[blk], m1s.at[0, blk], m1r.at[0, blk], right, h))
        m1_copies.append(rc(half(pacc.at[OP], blk, 1), m1_rt.at[blk], m1s.at[1, blk], m1r.at[1, blk], left, h))

    def bwd_body(i, carry):
        slot = lax.rem(i + 2, 3) + 1
        later = owner_of(slot) > c
        t2 = later.astype(jnp.int32)
        put(pacc.at[slot, 0], bwd(1 + 2 * slot, 1, slot, 0))
        pair = bwd(2 + 2 * slot, t2, slot, t2)

        @pl.when(later)
        def _():
            put(pacc.at[slot, 1], pair)

        @pl.when(jnp.logical_not(later))
        def _():
            add(pacc.at[slot, 0], pair)
            pacc[slot, 1] = jnp.zeros(pacc.shape[2:], F32)

        @pl.when(i == 0)
        def _():
            for cp in m1_copies:
                cp.start()

        @pl.when(i == 1)
        def _():
            for blk in range(2):
                m2copy(LF, blk, 0).start()

        @pl.when(i == 2)
        def _():
            for blk in range(2):
                m2copy(RT, blk, 1).start()
        return carry

    lax.fori_loop(0, 3, bwd_body, 0)
    put(pown.at[0], bwd(0, 0, OWN, 0))
    put(pown.at[1], bwd(1, 1, OWN, 1))
    add(pown.at[0], bwd(2, 1, OWN, 0))

    fo_copies = []
    for blk in range(2):
        src = pown.at[blk, pl.ds(off(blk, ho), seg), :]
        cp = rc(src, fin_own.at[blk], fos.at[0, blk], fos.at[1, blk], c, ho)
        cp.start()
        fo_copies.append(cp)

    for t in range(2):
        for g in range(groups):
            dq = (dqt[t, :, g * blk_len:(g + 1) * blk_len] * scale).astype(BF).T
            dq_tmp[g] = dq
        for g in range(groups):
            dq_send[g, t * seg:(t + 1) * seg, :] = dq_tmp[g, pl.ds(off(t, ho), seg), :]
            dq_rows[h * groups + g, t * seg:(t + 1) * seg, :] = dq_tmp[g, pl.ds(off(t, h), seg), :]
    dq_copy = rc(dq_send, dq_rows.at[pl.ds(h * groups, groups)], dqs, dqr, c, ho)
    dq_copy.start()

    for blk in range(2):
        for side, buf, slot in ((0, m1_lf, RT), (1, m1_rt, LF)):
            rc(buf.at[blk], buf.at[blk], m1s.at[side, blk], m1r.at[side, blk], left, h).wait_recv()
            pacc[slot, blk, side * seg:(side + 1) * seg, :] += buf[blk]
            m2copy(slot, blk, side).start()

    view = dq_rows.at[pl.ds(ho * groups, groups)]
    rc(dq_send, view, dqs, dqr, c, ho).wait_recv()
    for p in range(groups):
        a = 2 * p
        lhs = jnp.concatenate([dq_rows[a], dq_rows[a + 1]], axis=1)
        w = jnp.concatenate([wq_v[a], wq_v[a + 1]], axis=1)
        r = dot_nt(lhs, w)
        if p == 0:
            acc[...] = r
        else:
            acc[...] += r

    for blk in range(2):
        rc(fin_own.at[blk], fin_own.at[blk], fos.at[0, blk], fos.at[1, blk], c, ho).wait_recv()
        for side in range(2):
            for hh in range(2):
                dst = fin.at[side, hh, blk]
                rc(dst, dst, m2s.at[0, 0, 0], m2r.at[side, hh, blk], left, hh).wait_recv()
    for blk in range(2):
        r = pl.ds(blk * seg, seg)
        for hh, loc in ((h, pown[blk, pl.ds(off(blk, h), seg), :]), (ho, fin_own[blk])):
            tot = fin[0, hh, blk] + fin[1, hh, blk] + loc
            dkv[hh, r, :hd] = (tot[:, :hd] * scale).astype(BF)
            dkv[hh, r, hd:] = tot[:, hd:].astype(BF)
    out_v[...] = (acc[...] + dot_nt(dkv[0], wkv_v[0]) + dot_nt(dkv[1], wkv_v[1])).astype(BF)
    st = pltpu.make_async_copy(out_v, out_hbm, st_sem)
    st.start()

    for cp in kv_sends + dirs[0] + dirs[1] + q_sends + do_sends + relays + m1_copies + fo_copies + [dq_copy]:
        cp.wait_send()
    for slot in (LF, RT):
        for blk in range(2):
            for k in range(2):
                m2copy(slot, blk, k).wait_send()
    st.wait()


def solution(mesh):
    n_dev = mesh.shape["cp"]
    row_spec = P(("dp", "cp"), None)

    def device_fn(x_in, d_y, w_q, w_k, w_v, w_o):
        rows, d_model = x_in.shape
        q_heads, hd = w_q.shape[1], w_q.shape[2]
        kv_heads = w_k.shape[1]
        groups = q_heads // kv_heads
        seg = rows // 2
        blk = rows
        wq_t = jnp.transpose(w_q, (1, 0, 2))
        wk_r = w_k.reshape(d_model * kv_heads, hd)
        wv_r = w_v.reshape(d_model * kv_heads, hd)
        wo_r = w_o.reshape(q_heads * hd, d_model)
        vm = pltpu.VMEM
        dma = pltpu.SemaphoreType.DMA
        scratch = [
            vm((rows, d_model), BF), vm((rows, d_model), BF),
            vm((q_heads, d_model, hd), BF), vm((d_model * kv_heads, hd), BF), vm((d_model * kv_heads, hd), BF),
            vm((q_heads * hd, d_model), BF), vm((d_model * kv_heads, hd), F32), vm((kv_heads, d_model, 2 * hd), BF),
            vm((2, rows, 2 * hd), BF), vm((4, 2, blk, 2 * hd), BF),
            vm((groups, rows, hd), BF), vm((groups, rows, hd), BF),
            vm((2, groups, blk, hd), BF), vm((2, groups, blk, hd), BF),
            vm((9, groups, blk, blk), F32), vm((9, groups, blk, blk), F32),
            vm((2, groups, 1, blk), F32), vm((2, groups, 1, blk), F32), vm((2, groups, 1, blk), F32),
            vm((9, groups, 1, blk), F32),
            vm((blk, groups * blk), BF), vm((blk, groups * blk), BF), vm((2, hd, groups * blk), F32),
            vm((4, 2, blk, 2 * hd), F32), vm((2, blk, 2 * hd), F32),
            vm((2, seg, 2 * hd), F32), vm((2, seg, 2 * hd), F32),
            vm((2, 2, 2, seg, 2 * hd), F32), vm((2, seg, 2 * hd), F32),
            vm((groups, rows, hd), BF), vm((q_heads, rows, hd), BF), vm((rows, d_model), F32), vm((rows, d_model), BF),
            vm((2, rows, 2 * hd), BF), vm((groups, blk, hd), BF),
            dma((6,)), dma, dma((2, 2, 2)), dma((4, 2, 2)), dma((2,)), dma((2, 2)), dma((2, 2)), dma((2, 2)),
            dma((2, 2)), dma((2, 2)), dma((2, 2, 2)), dma((2, 2, 2)), dma((2, 2)), dma, dma,
        ]
        return pl.pallas_call(
            functools.partial(kernel, n_dev),
            out_shape=jax.ShapeDtypeStruct((rows, d_model), BF),
            in_specs=[pl.BlockSpec(memory_space=pl.ANY)] * 6,
            out_specs=pl.BlockSpec(memory_space=pl.ANY),
            scratch_shapes=scratch,
            compiler_params=pltpu.CompilerParams(collective_id=0, has_side_effects=True, vmem_limit_bytes=62 * 1024 * 1024),
        )(x_in, d_y, wq_t, wk_r, wv_r, wo_r)

    return jax.shard_map(device_fn, mesh=mesh, in_specs=(row_spec, row_spec, P(), P(), P(), P()), out_specs=row_spec, check_vma=False)
```

time: 164 us -> 41.6 us (0.25)
  the two profiles are of different devices: /device:TPU:112 before, /device:TPU:113 now
where the time goes in v1:
time: 41.6 us; the launch traced here: 41.5 us
  Pallas kernels  39.4 us (95%)
  local copies, waits for them, and re-layouts  2.06 us (5%)
    pallas_call x1, Pallas kernels, device_fn(): pl.pallas_call(functools.partial(kernel, n_dev), out_shape=jax.ShapeDtype...  39.4 us
    unnamed x1, local copies, waits for them, and re-layouts  2.06 us

profile of v1, /device:TPU:113, one launch (start us, length us, event | category | flops | bytes accessed | tf_op | source)
XLA Modules:
  0.0 41.5 jit_solution(8787672246375088504)
XLA Ops:
  0.0 39.4 %shard_map.64 = bf16[256,1536]{1,0:T(8,128)(2,1)} custom-call(bf16[256,1536]{1,0:T(8,128)(2,1)} %x_hbm.1, bf16[256,1536]{1,0:T(8,128)(2,1)} %dy_hbm.1, bf16[12,1536,128]{2,1,0:T(8,128)(2,1)} %bitcast.4, bf16[3072,128]{1,0:T(8,128)(2,1)} %bitcast.6, bf16[3072,128]{1,0:T(8,128)(2,1)} %bitcast.7, bf16[1536,1536]{1,0:T(8,128)(2,1)} %bitcast.5), custom_call_target="tpu_custom_call" | custom-call | tf_op jit(solution)/shard_map/pallas_call | solution.py:399
  39.4 2.1 %copy.8 = bf16[256,1536]{1,0:T(8,128)(2,1)} copy(bf16[256,1536]{1,0:T(8,128)(2,1)} %shard_map.64) | data formatting | bytes 1572864

commit v2 on v1

--- a/solution.py
+++ b/solution.py
@@ -23,12 +23,12 @@
     return lax.dot_general(a, b, NT, preferred_element_type=F32)
 
 
-def kernel(n_dev, x_hbm, dy_hbm, wq_hbm, wk_hbm, wv_hbm, wo_hbm, out_hbm,
+def kernel(n_dev, x_hbm, dy_hbm, wq_hbm, wk_hbm, wv_hbm, wo_hbm, out_v,
            x_v, dy_v, wq_v, wk_v, wv_v, wo_v, wf_v, wkv_v,
            kv_send, kvbuf, q_send, do_send, qbuf, dobuf,
            est, dpst, m_run, l_run, d_run, m_ent, p_buf, ds_buf, dqt,
-           pacc, pown, m1_lf, m1_rt, fin, fin_own, dq_send, dq_rows, acc, out_v, dkv, dq_tmp,
-           ld_sem, st_sem, kvs, kvr, kvps, kvrs, qs, qr, m1s, m1r, m2s, m2r, fos, dqs, dqr):
+           pacc, pown, m1_lf, m1_rt, fin, fin_own, dq_send, dq_rows, acc, dkv, dq_tmp, wkvt,
+           ld_sem, kvs, kvr, kvps, kvrs, qs, qr, m1s, m1r, m2s, m2r, fos, dqs, dqr):
     me = lax.axis_index("cp")
     n_chip = n_dev // 2
     c = me // 2
@@ -55,7 +55,7 @@
 
     loads = [pltpu.make_async_copy(a, b, ld_sem.at[i]) for i, (a, b) in enumerate([
         (wk_hbm, wk_v), (wv_hbm, wv_v), (x_hbm, x_v), (wq_hbm, wq_v), (dy_hbm, dy_v), (wo_hbm, wo_v)])]
-    for cp in loads:
+    for cp in loads[:3]:
         cp.start()
 
     barrier = pltpu.get_barrier_semaphore()
@@ -68,6 +68,8 @@
         for hh in range(2):
             wkv_v[hh, :, j * hd:(j + 1) * hd] = wf_v[pl.ds(hh, d_model, stride=2), :].astype(BF)
     loads[2].wait()
+    for cp in loads[3:]:
+        cp.start()
     for hh in range(2):
         kv_send[hh] = dot(x_v[...], wkv_v[hh]).astype(BF)
     for blk in range(2):
@@ -80,18 +82,16 @@
         kv_sends.append(rc(kv_send.at[ho, pl.ds(blk * seg, seg), :],
                            kvbuf.at[OWN, blk, pl.ds(off(blk, h), seg), :],
                            kvps.at[blk], kvr.at[OWN, h, blk], c, ho))
-    dirs = []
-    for first in range(2):
-        go_right = (h == first)
+    def kv_copies(d, hh):
+        go_right = (h == d)
         chip = jnp.where(go_right, right, left)
         slot = jnp.where(go_right, LF, RT)
-        dirs.append([rc(kv_send.at[hh, pl.ds(blk * seg, seg), :],
-                        kvbuf.at[slot, blk, pl.ds(off(blk, h), seg), :],
-                        kvs.at[first, hh, blk], kvr.at[slot, h, blk], chip, hh)
-                     for hh in range(2) for blk in range(2)])
-    for cp in dirs[0]:
-        cp.start()
-    for cp in kv_sends:
+        return [rc(kv_send.at[hh, pl.ds(blk * seg, seg), :],
+                   kvbuf.at[slot, blk, pl.ds(off(blk, h), seg), :],
+                   kvs.at[d, hh, blk], kvr.at[slot, h, blk], chip, hh) for blk in range(2)]
+
+    dirs = [kv_copies(0, 0), kv_copies(1, 0), kv_copies(0, 1), kv_copies(1, 1)]
+    for cp in dirs[0] + dirs[1] + dirs[2] + kv_sends:
         cp.start()
 
     def project(dst, src, grp, w_is_q):
@@ -126,8 +126,6 @@
     q_sends = xsends(q_send, qbuf, 0)
     for cp in q_sends:
         cp.start()
-    for cp in dirs[1]:
-        cp.start()
     project(to_own(qbuf), x_v, h, True)
     loads[4].wait()
     loads[5].wait()
@@ -136,17 +134,24 @@
     for cp in do_sends:
         cp.start()
 
-    relays = []
-    for core, slot, chip in ((0, LF, right), (1, RT, left)):
-        for blk in range(2):
-            view = kvbuf.at[slot, blk, pl.ds(off(blk, core), seg), :]
-            rc(view, view, kvs.at[0, 0, blk], kvr.at[slot, core, blk], chip, h).wait_recv()
-            cp = rc(view, kvbuf.at[OP, blk, pl.ds(off(blk, core), seg), :],
-                    kvrs.at[core, blk], kvr.at[OP, core, blk], chip, h)
-            cp.start()
-            relays.append(cp)
+    def relay(start):
+        cps = []
+        for core, slot, chip in ((0, LF, right), (1, RT, left)):
+            for blk in range(2):
+                view = kvbuf.at[slot, blk, pl.ds(off(blk, core), seg), :]
+                cp = rc(view, kvbuf.at[OP, blk, pl.ds(off(blk, core), seg), :],
+                        kvrs.at[core, blk], kvr.at[OP, core, blk], chip, h)
+                if start:
+                    rc(view, view, kvs.at[0, 0, blk], kvr.at[slot, core, blk], chip, h).wait_recv()
+                    cp.start()
+                cps.append(cp)
+        return cps
 
     project(to_own(dobuf), dy_v, h, False)
+
+    @pl.when(h == 0)
+    def _():
+        relay(True)
 
     def fwd(ent, t, slot, blk, diag, init):
         kv = kvbuf[slot, blk]
@@ -186,9 +191,17 @@
             rc(view, view, qs.at[k, t], qr.at[k, t], c, ho).wait_recv()
     for blk in range(2):
         wait_kv(OWN, ho, blk)
-    fwd(0, 0, OWN, 0, True, True)
+    m_run[0] = jnp.full(m_run.shape[1:], -jnp.inf, F32)
+    l_run[0] = jnp.zeros(l_run.shape[1:], F32)
+    d_run[0] = jnp.zeros(d_run.shape[1:], F32)
     fwd(1, 1, OWN, 1, True, True)
     fwd(2, 1, OWN, 0, False, False)
+    for cp in dirs[3]:
+        cp.start()
+
+    @pl.when(h == 1)
+    def _():
+        relay(True)
 
     def owner_of(slot):
         return jnp.where(slot == LF, left, jnp.where(slot == RT, right, opp))
@@ -208,6 +221,7 @@
 
         @pl.when(i == 2)
         def _():
+            fwd(0, 0, OWN, 0, True, False)
             for core in range(2):
                 for blk in range(2):
                     wait_kv(OP, core, blk)
@@ -251,6 +265,15 @@
     def half(ref, blk, k):
         return ref.at[blk, pl.ds(k * seg, seg), :]
 
+    def has(o, *chips):
+        return functools.reduce(jnp.logical_or, [o > x for x in chips])
+
+    def when(blk, cond, f):
+        if blk == 0:
+            f()
+        else:
+            pl.when(cond)(f)
+
     def m2copy(slot, blk, k):
         chip = right if slot == RT else left
         side = 0 if slot == RT else 1
@@ -268,6 +291,12 @@
         later = owner_of(slot) > c
         t2 = later.astype(jnp.int32)
         put(pacc.at[slot, 0], bwd(1 + 2 * slot, 1, slot, 0))
+
+        @pl.when(jnp.logical_and(i == 0, later))
+        def _():
+            for cp in m1_copies[:2]:
+                cp.start()
+
         pair = bwd(2 + 2 * slot, t2, slot, t2)
 
         @pl.when(later)
@@ -281,18 +310,25 @@
 
         @pl.when(i == 0)
         def _():
-            for cp in m1_copies:
-                cp.start()
+            @pl.when(later)
+            def _():
+                for cp in m1_copies[2:]:
+                    cp.start()
+
+            @pl.when(jnp.logical_not(later))
+            def _():
+                for cp in m1_copies[:2]:
+                    cp.start()
 
         @pl.when(i == 1)
         def _():
             for blk in range(2):
-                m2copy(LF, blk, 0).start()
+                when(blk, has(left, c), lambda: m2copy(LF, blk, 0).start())
 
         @pl.when(i == 2)
         def _():
             for blk in range(2):
-                m2copy(RT, blk, 1).start()
+                when(blk, has(right, c), lambda: m2copy(RT, blk, 1).start())
         return carry
 
     lax.fori_loop(0, 3, bwd_body, 0)
@@ -318,10 +354,12 @@
     dq_copy.start()
 
     for blk in range(2):
-        for side, buf, slot in ((0, m1_lf, RT), (1, m1_rt, LF)):
-            rc(buf.at[blk], buf.at[blk], m1s.at[side, blk], m1r.at[side, blk], left, h).wait_recv()
-            pacc[slot, blk, side * seg:(side + 1) * seg, :] += buf[blk]
-            m2copy(slot, blk, side).start()
+        for side, buf, slot, o, s in ((0, m1_lf, RT, right, left), (1, m1_rt, LF, left, right)):
+            def f():
+                rc(buf.at[blk], buf.at[blk], m1s.at[side, blk], m1r.at[side, blk], left, h).wait_recv()
+                pacc[slot, blk, side * seg:(side + 1) * seg, :] += buf[blk]
+            when(blk, has(o, s), f)
+            when(blk, has(o, s, c), lambda: m2copy(slot, blk, side).start())
 
     view = dq_rows.at[pl.ds(ho * groups, groups)]
     rc(dq_send, view, dqs, dqr, c, ho).wait_recv()
@@ -335,29 +373,41 @@
         else:
             acc[...] += r
 
+    for hh in range(2):
+        wkvt[hh] = wkv_v[hh].T
+
     for blk in range(2):
         rc(fin_own.at[blk], fin_own.at[blk], fos.at[0, blk], fos.at[1, blk], c, ho).wait_recv()
-        for side in range(2):
+        for side, s in ((0, left), (1, right)):
+            merged = (h if blk == 0 else 1 - h) == side
+            arrives = jnp.logical_or(has(c, s), jnp.logical_and(merged, has(c, opp)))
             for hh in range(2):
-                dst = fin.at[side, hh, blk]
-                rc(dst, dst, m2s.at[0, 0, 0], m2r.at[side, hh, blk], left, hh).wait_recv()
+                def f():
+                    dst = fin.at[side, hh, blk]
+                    rc(dst, dst, m2s.at[0, 0, 0], m2r.at[side, hh, blk], left, hh).wait_recv()
+                when(blk, arrives, f)
+                if blk == 1:
+                    @pl.when(jnp.logical_not(arrives))
+                    def _():
+                        fin[side, hh, blk] = jnp.zeros(fin.shape[3:], F32)
     for blk in range(2):
         r = pl.ds(blk * seg, seg)
         for hh, loc in ((h, pown[blk, pl.ds(off(blk, h), seg), :]), (ho, fin_own[blk])):
             tot = fin[0, hh, blk] + fin[1, hh, blk] + loc
             dkv[hh, r, :hd] = (tot[:, :hd] * scale).astype(BF)
             dkv[hh, r, hd:] = tot[:, hd:].astype(BF)
-    out_v[...] = (acc[...] + dot_nt(dkv[0], wkv_v[0]) + dot_nt(dkv[1], wkv_v[1])).astype(BF)
-    st = pltpu.make_async_copy(out_v, out_hbm, st_sem)
-    st.start()
-
-    for cp in kv_sends + dirs[0] + dirs[1] + q_sends + do_sends + relays + m1_copies + fo_copies + [dq_copy]:
+    out_v[...] = (acc[...] + dot(dkv[0], wkvt[0]) + dot(dkv[1], wkvt[1])).astype(BF)
+
+    for cp in kv_sends + sum(dirs, []) + q_sends + do_sends + relay(False) + fo_copies + [dq_copy]:
         cp.wait_send()
-    for slot in (LF, RT):
-        for blk in range(2):
-            for k in range(2):
-                m2copy(slot, blk, k).wait_send()
-    st.wait()
+    for blk in range(2):
+        def f():
+            for cp in m1_copies[2 * blk:2 * blk + 2]:
+                cp.wait_send()
+        when(blk, has(opp, c), f)
+        for slot, o, s, side in ((RT, right, left, 0), (LF, left, right, 1)):
+            when(blk, has(o, s, c), lambda: m2copy(slot, blk, side).wait_send())
+            when(blk, has(o, c), lambda: m2copy(slot, blk, 1 - side).wait_send())
 
 
 def solution(mesh):
@@ -391,18 +441,19 @@
             vm((4, 2, blk, 2 * hd), F32), vm((2, blk, 2 * hd), F32),
             vm((2, seg, 2 * hd), F32), vm((2, seg, 2 * hd), F32),
             vm((2, 2, 2, seg, 2 * hd), F32), vm((2, seg, 2 * hd), F32),
-            vm((groups, rows, hd), BF), vm((q_heads, rows, hd), BF), vm((rows, d_model), F32), vm((rows, d_model), BF),
-            vm((2, rows, 2 * hd), BF), vm((groups, blk, hd), BF),
-            dma((6,)), dma, dma((2, 2, 2)), dma((4, 2, 2)), dma((2,)), dma((2, 2)), dma((2, 2)), dma((2, 2)),
+            vm((groups, rows, hd), BF), vm((q_heads, rows, hd), BF), vm((rows, d_model), F32),
+            vm((2, rows, 2 * hd), BF), vm((groups, blk, hd), BF), vm((kv_heads, 2 * hd, d_model), BF),
+            dma((6,)), dma((2, 2, 2)), dma((4, 2, 2)), dma((2,)), dma((2, 2)), dma((2, 2)), dma((2, 2)),
             dma((2, 2)), dma((2, 2)), dma((2, 2, 2)), dma((2, 2, 2)), dma((2, 2)), dma, dma,
         ]
-        return pl.pallas_call(
+        res = pl.pallas_call(
             functools.partial(kernel, n_dev),
-            out_shape=jax.ShapeDtypeStruct((rows, d_model), BF),
+            out_shape=pltpu.VMEM((rows, d_model), BF),
             in_specs=[pl.BlockSpec(memory_space=pl.ANY)] * 6,
-            out_specs=pl.BlockSpec(memory_space=pl.ANY),
+            out_specs=pl.BlockSpec(memory_space=pltpu.VMEM),
             scratch_shapes=scratch,
             compiler_params=pltpu.CompilerParams(collective_id=0, has_side_effects=True, vmem_limit_bytes=62 * 1024 * 1024),
         )(x_in, d_y, wq_t, wk_r, wv_r, wo_r)
+        return res
 
     return jax.shard_map(device_fn, mesh=mesh, in_specs=(row_spec, row_spec, P(), P(), P(), P()), out_specs=row_spec, check_vma=False)

time: 41.6 us -> 38.5 us (0.925)
  the two profiles are of different devices: /device:TPU:113 before, /device:TPU:123 now
where the time goes in v2:
time: 38.5 us; the launch traced here: 38.4 us
  Pallas kernels  37.5 us (97%)
  local copies, waits for them, and re-layouts  0.88 us (2%)
    pallas_call x1, Pallas kernels, device_fn(): pl.pallas_call(functools.partial(kernel, n_dev), out_shape=pltpu.VMEM((ro...  37.5 us
    unnamed x1, local copies, waits for them, and re-layouts  0.88 us

profile of v2, /device:TPU:123, one launch (start us, length us, event | category | flops | bytes accessed | tf_op | source)
XLA Modules:
  0.0 38.4 jit_solution(5534327806798636979)
XLA Ops:
  0.0 37.5 %shard_map.64 = bf16[256,1536]{1,0:T(8,128)(2,1)S(1)} custom-call(bf16[256,1536]{1,0:T(8,128)(2,1)} %x_hbm.1, bf16[256,1536]{1,0:T(8,128)(2,1)} %dy_hbm.1, bf16[12,1536,128]{2,1,0:T(8,128)(2,1)} %bitcast.4, bf16[3072,128]{1,0:T(8,128)(2,1)} %bitcast.6, bf16[3072,128]{1,0:T(8,128)(2,1)} %bitcast.7, bf16[1536,1536]{1,0:T(8,128)(2,1)} %bitcast.5), custom_call_target="tpu_custom_call" | custom-call | tf_op jit(solution)/shard_map/pallas_call | solution.py:449
  37.5 0.9 %copy.8 = bf16[256,1536]{1,0:T(8,128)(2,1)} copy(bf16[256,1536]{1,0:T(8,128)(2,1)S(1)} %shard_map.64) | data formatting | bytes 1572864

commit v3 on v2

--- a/solution.py
+++ b/solution.py
@@ -53,22 +53,28 @@
         return pltpu.make_async_remote_copy(src_ref=src, dst_ref=dst, send_sem=ssem, recv_sem=rsem,
                                             device_id={"cp": chip * 2 + core}, device_id_type=MESH)
 
-    loads = [pltpu.make_async_copy(a, b, ld_sem.at[i]) for i, (a, b) in enumerate([
-        (wk_hbm, wk_v), (wv_hbm, wv_v), (x_hbm, x_v), (wq_hbm, wq_v), (dy_hbm, dy_v), (wo_hbm, wo_v)])]
-    for cp in loads[:3]:
+    def load(i, src, dst):
+        return pltpu.make_async_copy(src, dst, ld_sem.at[i])
+
+    ld_k, ld_v, ld_x = load(0, wk_hbm, wk_v), load(1, wv_hbm, wv_v), load(2, x_hbm, x_v)
+    ld_q, ld_y, ld_o = load(3, wq_hbm, wq_v), load(4, dy_hbm, dy_v), load(5, wo_hbm, wo_v)
+    for cp in (ld_k, ld_v, ld_x, ld_q):
         cp.start()
 
     barrier = pltpu.get_barrier_semaphore()
     for chip, core in ((c, ho), (right, 0), (right, 1), (left, 0), (left, 1)):
         pl.semaphore_signal(barrier, inc=1, device_id={"cp": chip * 2 + core}, device_id_type=MESH)
 
-    for j, (ld, w) in enumerate(((loads[0], wk_v), (loads[1], wv_v))):
+    for j, (ld, w) in enumerate(((ld_k, wk_v), (ld_v, wv_v))):
         ld.wait()
+        if j == 0:
+            for cp in (ld_y, ld_o):
+                cp.start()
         wf_v[...] = w[...].astype(F32)
         for hh in range(2):
             wkv_v[hh, :, j * hd:(j + 1) * hd] = wf_v[pl.ds(hh, d_model, stride=2), :].astype(BF)
-    loads[2].wait()
-    for cp in loads[3:]:
+    ld_x.wait()
+    for cp in ():
         cp.start()
     for hh in range(2):
         kv_send[hh] = dot(x_v[...], wkv_v[hh]).astype(BF)
@@ -91,7 +97,7 @@
                    kvs.at[d, hh, blk], kvr.at[slot, h, blk], chip, hh) for blk in range(2)]
 
     dirs = [kv_copies(0, 0), kv_copies(1, 0), kv_copies(0, 1), kv_copies(1, 1)]
-    for cp in dirs[0] + dirs[1] + dirs[2] + kv_sends:
+    for cp in dirs[0] + dirs[1] + kv_sends:
         cp.start()
 
     def project(dst, src, grp, w_is_q):
@@ -121,18 +127,21 @@
         return [rc(buf.at[:, pl.ds(t * seg, seg), :], dst.at[t, :, pl.ds(off(t, h), seg), :],
                    qs.at[k, t], qr.at[k, t], c, ho) for t in range(2)]
 
-    loads[3].wait()
+    ld_q.wait()
     project(to_send(q_send), x_v, ho, True)
     q_sends = xsends(q_send, qbuf, 0)
     for cp in q_sends:
         cp.start()
     project(to_own(qbuf), x_v, h, True)
-    loads[4].wait()
-    loads[5].wait()
+    for cp in dirs[2] + dirs[3]:
+        cp.start()
+    ld_y.wait()
+    ld_o.wait()
     project(to_send(do_send), dy_v, ho, False)
     do_sends = xsends(do_send, dobuf, 1)
     for cp in do_sends:
         cp.start()
+    project(to_own(dobuf), dy_v, h, False)
 
     def relay(start):
         cps = []
@@ -146,8 +155,6 @@
                     cp.start()
                 cps.append(cp)
         return cps
-
-    project(to_own(dobuf), dy_v, h, False)
 
     @pl.when(h == 0)
     def _():
@@ -196,8 +203,9 @@
     d_run[0] = jnp.zeros(d_run.shape[1:], F32)
     fwd(1, 1, OWN, 1, True, True)
     fwd(2, 1, OWN, 0, False, False)
-    for cp in dirs[3]:
-        cp.start()
+    @pl.when(h == 1)
+    def _():
+        fwd(0, 0, OWN, 0, True, False)
 
     @pl.when(h == 1)
     def _():
@@ -221,7 +229,6 @@
 
         @pl.when(i == 2)
         def _():
-            fwd(0, 0, OWN, 0, True, False)
             for core in range(2):
                 for blk in range(2):
                     wait_kv(OP, core, blk)
@@ -233,11 +240,13 @@
 
     lax.fori_loop(0, 3, fwd_body, 0)
 
-    for t in range(2):
+    def finish(t):
         for g in range(groups):
             l = l_run[t, g]
             d_run[t, g] = d_run[t, g] / l
             m_run[t, g] = m_run[t, g] + jnp.log2(l)
+
+    finish(1)
 
     dqt[...] = jnp.zeros_like(dqt)
 
@@ -296,6 +305,13 @@
         def _():
             for cp in m1_copies[:2]:
                 cp.start()
+
+        @pl.when(i == 0)
+        def _():
+            @pl.when(h == 0)
+            def _():
+                fwd(0, 0, OWN, 0, True, False)
+            finish(0)
 
         pair = bwd(2 + 2 * slot, t2, slot, t2)
 

time: 38.5 us -> 36.8 us (0.956)
  Pallas kernels: 37.5 us -> 35.9 us
    pallas_call x1, Pallas kernels: 37.5 us -> 35.9 us  [device_fn(): pl.pallas_call(functools.partial(kernel, n_dev), out_shape=pltpu.VMEM((ro...]
where the time goes in v3:
time: 36.8 us
  Pallas kernels  35.9 us (98%)
  local copies, waits for them, and re-layouts  0.88 us (2%)
    pallas_call x1, Pallas kernels, device_fn(): pl.pallas_call(functools.partial(kernel, n_dev), out_shape=pltpu.VMEM((ro...  35.9 us
    unnamed x1, local copies, waits for them, and re-layouts  0.88 us

profile of v3, /device:TPU:123, one launch (start us, length us, event | category | flops | bytes accessed | tf_op | source)
XLA Modules:
  0.0 36.8 jit_solution(9371911434437900998)
XLA Ops:
  0.0 35.9 %shard_map.64 = bf16[256,1536]{1,0:T(8,128)(2,1)S(1)} custom-call(bf16[256,1536]{1,0:T(8,128)(2,1)} %x_hbm.1, bf16[256,1536]{1,0:T(8,128)(2,1)} %dy_hbm.1, bf16[12,1536,128]{2,1,0:T(8,128)(2,1)} %bitcast.4, bf16[3072,128]{1,0:T(8,128)(2,1)} %bitcast.6, bf16[3072,128]{1,0:T(8,128)(2,1)} %bitcast.7, bf16[1536,1536]{1,0:T(8,128)(2,1)} %bitcast.5), custom_call_target="tpu_custom_call" | custom-call | tf_op jit(solution)/shard_map/pallas_call | solution.py:465
  35.9 0.9 %copy.8 = bf16[256,1536]{1,0:T(8,128)(2,1)} copy(bf16[256,1536]{1,0:T(8,128)(2,1)S(1)} %shard_map.64) | data formatting | bytes 1572864

commit v4 on v3

--- a/solution.py
+++ b/solution.py
@@ -12,6 +12,7 @@
 BF = jnp.bfloat16
 F32 = jnp.float32
 OWN, LF, RT, OP = 0, 1, 2, 3
+MERGE_EARLY = True
 NT = (((1,), (1,)), ((), ()))
 
 
@@ -57,7 +58,11 @@
         return pltpu.make_async_copy(src, dst, ld_sem.at[i])
 
     ld_k, ld_v, ld_x = load(0, wk_hbm, wk_v), load(1, wv_hbm, wv_v), load(2, x_hbm, x_v)
-    ld_q, ld_y, ld_o = load(3, wq_hbm, wq_v), load(4, dy_hbm, dy_v), load(5, wo_hbm, wo_v)
+    ld_q, ld_y = load(3, wq_hbm, wq_v), load(4, dy_hbm, dy_v)
+    ld_o = []
+    for i, grp in enumerate((ho, h)):
+        r = pl.ds(pl.multiple_of(grp * groups * hd, hd), groups * hd)
+        ld_o.append(load(5 + i, wo_hbm.at[r], wo_v.at[r]))
     for cp in (ld_k, ld_v, ld_x, ld_q):
         cp.start()
 
@@ -68,26 +73,19 @@
     for j, (ld, w) in enumerate(((ld_k, wk_v), (ld_v, wv_v))):
         ld.wait()
         if j == 0:
-            for cp in (ld_y, ld_o):
+            for cp in [ld_y] + ld_o:
                 cp.start()
-        wf_v[...] = w[...].astype(F32)
-        for hh in range(2):
-            wkv_v[hh, :, j * hd:(j + 1) * hd] = wf_v[pl.ds(hh, d_model, stride=2), :].astype(BF)
+        wf_v[j] = w[...].astype(F32)
     ld_x.wait()
-    for cp in ():
-        cp.start()
-    for hh in range(2):
+
+    def project_kv(hh):
+        for j in range(2):
+            wkv_v[hh, :, j * hd:(j + 1) * hd] = wf_v[j, pl.ds(hh, d_model, stride=2), :].astype(BF)
         kv_send[hh] = dot(x_v[...], wkv_v[hh]).astype(BF)
-    for blk in range(2):
-        kvbuf[OWN, blk, pl.ds(off(blk, h), seg), :] = kv_send[h, blk * seg:(blk + 1) * seg, :]
-
+
+    project_kv(0)
     pl.semaphore_wait(barrier, 5)
 
-    kv_sends = []
-    for blk in range(2):
-        kv_sends.append(rc(kv_send.at[ho, pl.ds(blk * seg, seg), :],
-                           kvbuf.at[OWN, blk, pl.ds(off(blk, h), seg), :],
-                           kvps.at[blk], kvr.at[OWN, h, blk], c, ho))
     def kv_copies(d, hh):
         go_right = (h == d)
         chip = jnp.where(go_right, right, left)
@@ -97,7 +95,17 @@
                    kvs.at[d, hh, blk], kvr.at[slot, h, blk], chip, hh) for blk in range(2)]
 
     dirs = [kv_copies(0, 0), kv_copies(1, 0), kv_copies(0, 1), kv_copies(1, 1)]
-    for cp in dirs[0] + dirs[1] + kv_sends:
+    for cp in dirs[0] + dirs[1]:
+        cp.start()
+    project_kv(1)
+    for blk in range(2):
+        kvbuf[OWN, blk, pl.ds(off(blk, h), seg), :] = kv_send[h, blk * seg:(blk + 1) * seg, :]
+    kv_sends = []
+    for blk in range(2):
+        kv_sends.append(rc(kv_send.at[ho, pl.ds(blk * seg, seg), :],
+                           kvbuf.at[OWN, blk, pl.ds(off(blk, h), seg), :],
+                           kvps.at[blk], kvr.at[OWN, h, blk], c, ho))
+    for cp in kv_sends:
         cp.start()
 
     def project(dst, src, grp, w_is_q):
@@ -132,15 +140,18 @@
     q_sends = xsends(q_send, qbuf, 0)
     for cp in q_sends:
         cp.start()
+    for cp in dirs[2]:
+        cp.start()
     project(to_own(qbuf), x_v, h, True)
-    for cp in dirs[2] + dirs[3]:
+    for cp in dirs[3]:
         cp.start()
     ld_y.wait()
-    ld_o.wait()
+    ld_o[0].wait()
     project(to_send(do_send), dy_v, ho, False)
     do_sends = xsends(do_send, dobuf, 1)
     for cp in do_sends:
         cp.start()
+    ld_o[1].wait()
     project(to_own(dobuf), dy_v, h, False)
 
     def relay(start):
@@ -257,12 +268,13 @@
             p_buf[:, g * blk_len:(g + 1) * blk_len] = p
             ds_buf[:, g * blk_len:(g + 1) * blk_len] = (
                 p.astype(F32) * (dpst[ent, g] - d_run[t, g])).astype(BF)
-        kt = kvbuf[slot, blk][:, :hd].T
-        dqt[t] += dot(kt, ds_buf[...])
         dk = dot(ds_buf[...], qbuf[t].reshape(groups * blk_len, hd))
         dv = dot(p_buf[...], dobuf[t].reshape(groups * blk_len, hd))
         return dk, dv
 
+    def bwd_q(t, slot, blk):
+        dqt[t] += dot(kvbuf[slot, blk][:, :hd].T, ds_buf[...])
+
     def put(ref, pair):
         ref[:, :hd] = pair[0]
         ref[:, hd:] = pair[1]
@@ -274,83 +286,130 @@
     def half(ref, blk, k):
         return ref.at[blk, pl.ds(k * seg, seg), :]
 
-    def has(o, *chips):
-        return functools.reduce(jnp.logical_or, [o > x for x in chips])
-
-    def when(blk, cond, f):
-        if blk == 0:
-            f()
+    def con(blk, o, s):
+        return jnp.logical_or(blk == 0, o > s)
+
+    def via_left(s):
+        return s != 0
+
+    def meets(slot, blk, k, o, s):
+        if blk == 0 or k == 1:
+            here = (k == 0) == (slot == RT)
         else:
-            pl.when(cond)(f)
+            here = via_left(s) if slot == LF else jnp.logical_not(via_left(s))
+        return jnp.logical_and(con(blk, o, s), here)
 
     def m2copy(slot, blk, k):
         chip = right if slot == RT else left
         side = 0 if slot == RT else 1
         core = k if blk == 0 else 1 - k
-        return rc(half(pacc.at[slot], blk, k), fin.at[side, h, blk], m2s.at[side, blk, k],
+        return rc(half(pacc.at[slot - 1], blk, k), fin.at[side, h, blk], m2s.at[side, blk, k],
                   m2r.at[side, h, blk], chip, core)
 
-    m1_copies = []
-    for blk in range(2):
-        m1_copies.append(rc(half(pacc.at[OP], blk, 0), m1_lf.at[blk], m1s.at[0, blk], m1r.at[0, blk], right, h))
-        m1_copies.append(rc(half(pacc.at[OP], blk, 1), m1_rt.at[blk], m1s.at[1, blk], m1r.at[1, blk], left, h))
+    def m1(blk, k, d):
+        j = 2 if (k == 0 and d == 1) else blk
+        return rc(half(pacc.at[OP - 1], blk, k), (m1_lf, m1_rt)[d].at[j], m1s.at[d, j], m1r.at[d, j], (right, left)[d], h)
+
+    def m1_each(blk, f):
+        @pl.when(con(blk, opp, c))
+        def _():
+            f(m1(blk, 1, 1))
+            if blk == 0:
+                f(m1(0, 0, 0))
+            else:
+                for d, ok in enumerate((jnp.logical_not(via_left(c)), via_left(c))):
+                    @pl.when(ok)
+                    def _():
+                        f(m1(1, 0, d))
+
+    def direct_each(slot, blk, f):
+        o, s = (right, left) if slot == RT else (left, right)
+        for k in range(2):
+            @pl.when(jnp.logical_and(con(blk, o, c), jnp.logical_not(meets(slot, blk, k, o, s))))
+            def _():
+                f(m2copy(slot, blk, k))
+
+    def merged_each(f):
+        for blk in range(2):
+            for slot, o, s in ((RT, right, left), (LF, left, right)):
+                for k in range(2):
+                    if (blk == 0 or k == 1) and (k == 0) != (slot == RT):
+                        continue
+                    d = 0 if slot == RT else 1
+                    j = 2 if (k == 0 and d == 1) else blk
+
+                    @pl.when(meets(slot, blk, k, o, s))
+                    def _():
+                        f((m1_lf, m1_rt)[d].at[j], m1r.at[d, j], slot, blk, k)
+
+    first_chip = jnp.logical_not(functools.reduce(jnp.logical_or, [c > x for x in (left, right, opp)]))
+
+    def low_block():
+        @pl.when(h == 0)
+        def _():
+            fwd(0, 0, OWN, 0, True, False)
+        finish(0)
 
     def bwd_body(i, carry):
-        slot = lax.rem(i + 2, 3) + 1
-        later = owner_of(slot) > c
-        t2 = later.astype(jnp.int32)
-        put(pacc.at[slot, 0], bwd(1 + 2 * slot, 1, slot, 0))
-
-        @pl.when(jnp.logical_and(i == 0, later))
-        def _():
-            for cp in m1_copies[:2]:
-                cp.start()
-
-        @pl.when(i == 0)
-        def _():
-            @pl.when(h == 0)
+        for j in range(2):
+            near = (LF, RT)[j]
+            slot = jnp.where(i == 0, OP, near)
+            second = (i == 2) if j == 0 else (i != 1)
+            later = owner_of(slot) > c
+            t = jnp.where(second, later.astype(jnp.int32), 1)
+            blk = jnp.where(second, later.astype(jnp.int32), 0)
+            fresh = jnp.logical_or(jnp.logical_not(second), later)
+            ready = jnp.where(second, True, later)
+            pair = bwd(1 + 2 * slot + second.astype(jnp.int32), t, slot, blk)
+
+            @pl.when(fresh)
             def _():
-                fwd(0, 0, OWN, 0, True, False)
-            finish(0)
-
-        pair = bwd(2 + 2 * slot, t2, slot, t2)
-
-        @pl.when(later)
-        def _():
-            put(pacc.at[slot, 1], pair)
-
-        @pl.when(jnp.logical_not(later))
-        def _():
-            add(pacc.at[slot, 0], pair)
-            pacc[slot, 1] = jnp.zeros(pacc.shape[2:], F32)
-
-        @pl.when(i == 0)
-        def _():
-            @pl.when(later)
+                put(pacc.at[slot - 1, blk], pair)
+
+            @pl.when(jnp.logical_not(fresh))
             def _():
-                for cp in m1_copies[2:]:
-                    cp.start()
-
-            @pl.when(jnp.logical_not(later))
-            def _():
-                for cp in m1_copies[:2]:
-                    cp.start()
-
-        @pl.when(i == 1)
-        def _():
-            for blk in range(2):
-                when(blk, has(left, c), lambda: m2copy(LF, blk, 0).start())
-
-        @pl.when(i == 2)
-        def _():
-            for blk in range(2):
-                when(blk, has(right, c), lambda: m2copy(RT, blk, 1).start())
+                add(pacc.at[slot - 1, 0], pair)
+                pacc[slot - 1, 1] = jnp.zeros(pacc.shape[2:], F32)
+
+            for bb in range(2):
+                @pl.when(jnp.logical_and(ready, blk == bb))
+                def _():
+                    @pl.when(i == 0)
+                    def _():
+                        m1_each(bb, lambda cp: cp.start())
+
+                    @pl.when(i != 0)
+                    def _():
+                        direct_each(near, bb, lambda cp: cp.start())
+
+            bwd_q(t, slot, blk)
+
+            if j == 0:
+                @pl.when(jnp.logical_and(i == 0, jnp.logical_not(first_chip)))
+                def _():
+                    low_block()
         return carry
 
     lax.fori_loop(0, 3, bwd_body, 0)
+
+    def merge(buf, sem, slot, blk, k):
+        rc(buf, buf, m1s.at[0, 0], sem, left, h).wait_recv()
+        pacc[slot - 1, blk, k * seg:(k + 1) * seg, :] += buf[...]
+        m2copy(slot, blk, k).start()
+
+    if MERGE_EARLY:
+        merged_each(merge)
+
+    @pl.when(first_chip)
+    def _():
+        low_block()
+
     put(pown.at[0], bwd(0, 0, OWN, 0))
+    bwd_q(0, OWN, 0)
     put(pown.at[1], bwd(1, 1, OWN, 1))
+    bwd_q(1, OWN, 1)
     add(pown.at[0], bwd(2, 1, OWN, 0))
+    bwd_q(1, OWN, 0)
 
     fo_copies = []
     for blk in range(2):
@@ -369,13 +428,8 @@
     dq_copy = rc(dq_send, dq_rows.at[pl.ds(h * groups, groups)], dqs, dqr, c, ho)
     dq_copy.start()
 
-    for blk in range(2):
-        for side, buf, slot, o, s in ((0, m1_lf, RT, right, left), (1, m1_rt, LF, left, right)):
-            def f():
-                rc(buf.at[blk], buf.at[blk], m1s.at[side, blk], m1r.at[side, blk], left, h).wait_recv()
-                pacc[slot, blk, side * seg:(side + 1) * seg, :] += buf[blk]
-            when(blk, has(o, s), f)
-            when(blk, has(o, s, c), lambda: m2copy(slot, blk, side).start())
+    if not MERGE_EARLY:
+        merged_each(merge)
 
     view = dq_rows.at[pl.ds(ho * groups, groups)]
     rc(dq_send, view, dqs, dqr, c, ho).wait_recv()
@@ -394,18 +448,24 @@
 
     for blk in range(2):
         rc(fin_own.at[blk], fin_own.at[blk], fos.at[0, blk], fos.at[1, blk], c, ho).wait_recv()
-        for side, s in ((0, left), (1, right)):
-            merged = (h if blk == 0 else 1 - h) == side
-            arrives = jnp.logical_or(has(c, s), jnp.logical_and(merged, has(c, opp)))
+        k = h if blk == 0 else 1 - h
+        for side, nb in ((0, left), (1, right)):
+            if blk == 0:
+                way = True
+            elif side == 0:
+                way = jnp.logical_and(k == 0, jnp.logical_not(via_left(opp)))
+            else:
+                way = jnp.logical_or(k == 1, via_left(opp))
+            arrives = jnp.logical_or(con(blk, c, nb), jnp.logical_and(con(blk, c, opp), way))
             for hh in range(2):
-                def f():
+                @pl.when(arrives)
+                def _():
                     dst = fin.at[side, hh, blk]
                     rc(dst, dst, m2s.at[0, 0, 0], m2r.at[side, hh, blk], left, hh).wait_recv()
-                when(blk, arrives, f)
-                if blk == 1:
-                    @pl.when(jnp.logical_not(arrives))
-                    def _():
-                        fin[side, hh, blk] = jnp.zeros(fin.shape[3:], F32)
+
+                @pl.when(jnp.logical_not(arrives))
+                def _():
+                    fin[side, hh, blk] = jnp.zeros(fin.shape[3:], F32)
     for blk in range(2):
         r = pl.ds(blk * seg, seg)
         for hh, loc in ((h, pown[blk, pl.ds(off(blk, h), seg), :]), (ho, fin_own[blk])):
@@ -417,13 +477,11 @@
     for cp in kv_sends + sum(dirs, []) + q_sends + do_sends + relay(False) + fo_copies + [dq_copy]:
         cp.wait_send()
     for blk in range(2):
-        def f():
-            for cp in m1_copies[2 * blk:2 * blk + 2]:
-                cp.wait_send()
-        when(blk, has(opp, c), f)
-        for slot, o, s, side in ((RT, right, left, 0), (LF, left, right, 1)):
-            when(blk, has(o, s, c), lambda: m2copy(slot, blk, side).wait_send())
-            when(blk, has(o, c), lambda: m2copy(slot, blk, 1 - side).wait_send())
+        m1_each(blk, lambda cp: cp.wait_send())
+    for slot in (LF, RT):
+        for blk in range(2):
+            direct_each(slot, blk, lambda cp: cp.wait_send())
+    merged_each(lambda buf, sem, slot, blk, k: m2copy(slot, blk, k).wait_send())
 
 
 def solution(mesh):
@@ -446,7 +504,7 @@
         scratch = [
             vm((rows, d_model), BF), vm((rows, d_model), BF),
             vm((q_heads, d_model, hd), BF), vm((d_model * kv_heads, hd), BF), vm((d_model * kv_heads, hd), BF),
-            vm((q_heads * hd, d_model), BF), vm((d_model * kv_heads, hd), F32), vm((kv_heads, d_model, 2 * hd), BF),
+            vm((q_heads * hd, d_model), BF), vm((2, d_model * kv_heads, hd), F32), vm((kv_heads, d_model, 2 * hd), BF),
             vm((2, rows, 2 * hd), BF), vm((4, 2, blk, 2 * hd), BF),
             vm((groups, rows, hd), BF), vm((groups, rows, hd), BF),
             vm((2, groups, blk, hd), BF), vm((2, groups, blk, hd), BF),
@@ -454,13 +512,13 @@
             vm((2, groups, 1, blk), F32), vm((2, groups, 1, blk), F32), vm((2, groups, 1, blk), F32),
             vm((9, groups, 1, blk), F32),
             vm((blk, groups * blk), BF), vm((blk, groups * blk), BF), vm((2, hd, groups * blk), F32),
-            vm((4, 2, blk, 2 * hd), F32), vm((2, blk, 2 * hd), F32),
-            vm((2, seg, 2 * hd), F32), vm((2, seg, 2 * hd), F32),
+            vm((3, 2, blk, 2 * hd), F32), vm((2, blk, 2 * hd), F32),
+            vm((2, seg, 2 * hd), F32), vm((3, seg, 2 * hd), F32),
             vm((2, 2, 2, seg, 2 * hd), F32), vm((2, seg, 2 * hd), F32),
             vm((groups, rows, hd), BF), vm((q_heads, rows, hd), BF), vm((rows, d_model), F32),
             vm((2, rows, 2 * hd), BF), vm((groups, blk, hd), BF), vm((kv_heads, 2 * hd, d_model), BF),
-            dma((6,)), dma((2, 2, 2)), dma((4, 2, 2)), dma((2,)), dma((2, 2)), dma((2, 2)), dma((2, 2)),
-            dma((2, 2)), dma((2, 2)), dma((2, 2, 2)), dma((2, 2, 2)), dma((2, 2)), dma, dma,
+            dma((7,)), dma((2, 2, 2)), dma((4, 2, 2)), dma((2,)), dma((2, 2)), dma((2, 2)), dma((2, 2)),
+            dma((2, 3)), dma((2, 3)), dma((2, 2, 2)), dma((2, 2, 2)), dma((2, 2)), dma, dma,
         ]
         res = pl.pallas_call(
             functools.partial(kernel, n_dev),
@@ -468,7 +526,7 @@
             in_specs=[pl.BlockSpec(memory_space=pl.ANY)] * 6,
             out_specs=pl.BlockSpec(memory_space=pltpu.VMEM),
             scratch_shapes=scratch,
-            compiler_params=pltpu.CompilerParams(collective_id=0, has_side_effects=True, vmem_limit_bytes=62 * 1024 * 1024),
+            compiler_params=pltpu.CompilerParams(collective_id=0, has_side_effects=True, vmem_limit_bytes=63 * 1024 * 1024),
         )(x_in, d_y, wq_t, wk_r, wv_r, wo_r)
         return res
 

time: 36.8 us -> 36.6 us (level)
  the two profiles are of different devices: /device:TPU:123 before, /device:TPU:122 now
where the time goes in v4:
time: 36.6 us; the launch traced here: 36.5 us
  Pallas kernels  35.6 us (97%)
  local copies, waits for them, and re-layouts  0.88 us (2%)
    pallas_call x1, Pallas kernels, device_fn(): pl.pallas_call(functools.partial(kernel, n_dev), out_shape=pltpu.VMEM((ro...  35.6 us
    unnamed x1, local copies, waits for them, and re-layouts  0.88 us

profile of v4, /device:TPU:122, one launch (start us, length us, event | category | flops | bytes accessed | tf_op | source)
XLA Modules:
  0.0 36.5 jit_solution(9723308774340416638)
XLA Ops:
  0.0 35.6 %shard_map.64 = bf16[256,1536]{1,0:T(8,128)(2,1)S(1)} custom-call(bf16[256,1536]{1,0:T(8,128)(2,1)} %x_hbm.1, bf16[256,1536]{1,0:T(8,128)(2,1)} %dy_hbm.1, bf16[12,1536,128]{2,1,0:T(8,128)(2,1)} %bitcast.4, bf16[3072,128]{1,0:T(8,128)(2,1)} %bitcast.6, bf16[3072,128]{1,0:T(8,128)(2,1)} %bitcast.7, bf16[1536,1536]{1,0:T(8,128)(2,1)} %bitcast.5), custom_call_target="tpu_custom_call" | custom-call | tf_op jit(solution)/shard_map/pallas_call | solution.py:523
  35.6 0.9 %copy.8 = bf16[256,1536]{1,0:T(8,128)(2,1)} copy(bf16[256,1536]{1,0:T(8,128)(2,1)S(1)} %shard_map.64) | data formatting | bytes 1572864

commit v5 on v4

--- a/solution.py
+++ b/solution.py
@@ -446,18 +446,18 @@
     for hh in range(2):
         wkvt[hh] = wkv_v[hh].T
 
-    for blk in range(2):
-        rc(fin_own.at[blk], fin_own.at[blk], fos.at[0, blk], fos.at[1, blk], c, ho).wait_recv()
-        k = h if blk == 0 else 1 - h
-        for side, nb in ((0, left), (1, right)):
-            if blk == 0:
-                way = True
-            elif side == 0:
-                way = jnp.logical_and(k == 0, jnp.logical_not(via_left(opp)))
-            else:
-                way = jnp.logical_or(k == 1, via_left(opp))
-            arrives = jnp.logical_or(con(blk, c, nb), jnp.logical_and(con(blk, c, opp), way))
-            for hh in range(2):
+    for hh in range(2):
+        for blk in range(2):
+            k = h if blk == 0 else 1 - h
+            for side, nb in ((0, left), (1, right)):
+                if blk == 0:
+                    way = True
+                elif side == 0:
+                    way = jnp.logical_and(k == 0, jnp.logical_not(via_left(opp)))
+                else:
+                    way = jnp.logical_or(k == 1, via_left(opp))
+                arrives = jnp.logical_or(con(blk, c, nb), jnp.logical_and(con(blk, c, opp), way))
+
                 @pl.when(arrives)
                 def _():
                     dst = fin.at[side, hh, blk]
@@ -466,13 +466,28 @@
                 @pl.when(jnp.logical_not(arrives))
                 def _():
                     fin[side, hh, blk] = jnp.zeros(fin.shape[3:], F32)
-    for blk in range(2):
-        r = pl.ds(blk * seg, seg)
-        for hh, loc in ((h, pown[blk, pl.ds(off(blk, h), seg), :]), (ho, fin_own[blk])):
+
+        def total(blk, loc):
+            r = pl.ds(blk * seg, seg)
             tot = fin[0, hh, blk] + fin[1, hh, blk] + loc
             dkv[hh, r, :hd] = (tot[:, :hd] * scale).astype(BF)
             dkv[hh, r, hd:] = tot[:, hd:].astype(BF)
-    out_v[...] = (acc[...] + dot(dkv[0], wkvt[0]) + dot(dkv[1], wkvt[1])).astype(BF)
+
+        @pl.when(h == hh)
+        def _():
+            for blk in range(2):
+                total(blk, pown[blk, pl.ds(off(blk, h), seg), :])
+
+        @pl.when(h != hh)
+        def _():
+            for blk in range(2):
+                rc(fin_own.at[blk], fin_own.at[blk], fos.at[0, blk], fos.at[1, blk], c, ho).wait_recv()
+                total(blk, fin_own[blk])
+
+        if hh == 0:
+            acc[...] += dot(dkv[0], wkvt[0])
+        else:
+            out_v[...] = (acc[...] + dot(dkv[1], wkvt[1])).astype(BF)
 
     for cp in kv_sends + sum(dirs, []) + q_sends + do_sends + relay(False) + fo_copies + [dq_copy]:
         cp.wait_send()

time: 36.6 us -> 36.4 us (level)
  no operation moved by 1% of the time
where the time goes in v5:
time: 36.4 us; the launch traced here: 36.3 us
  Pallas kernels  35.4 us (97%)
  local copies, waits for them, and re-layouts  0.88 us (2%)
    pallas_call x1, Pallas kernels, device_fn(): pl.pallas_call(functools.partial(kernel, n_dev), out_shape=pltpu.VMEM((ro...  35.4 us
    unnamed x1, local copies, waits for them, and re-layouts  0.88 us

profile of v5, /device:TPU:122, one launch (start us, length us, event | category | flops | bytes accessed | tf_op | source)
XLA Modules:
  0.0 36.3 jit_solution(4291522944271707890)
XLA Ops:
  0.0 35.4 %shard_map.64 = bf16[256,1536]{1,0:T(8,128)(2,1)S(1)} custom-call(bf16[256,1536]{1,0:T(8,128)(2,1)} %x_hbm.1, bf16[256,1536]{1,0:T(8,128)(2,1)} %dy_hbm.1, bf16[12,1536,128]{2,1,0:T(8,128)(2,1)} %bitcast.4, bf16[3072,128]{1,0:T(8,128)(2,1)} %bitcast.6, bf16[3072,128]{1,0:T(8,128)(2,1)} %bitcast.7, bf16[1536,1536]{1,0:T(8,128)(2,1)} %bitcast.5), custom_call_target="tpu_custom_call" | custom-call | tf_op jit(solution)/shard_map/pallas_call | solution.py:538
  35.4 0.9 %copy.8 = bf16[256,1536]{1,0:T(8,128)(2,1)} copy(bf16[256,1536]{1,0:T(8,128)(2,1)S(1)} %shard_map.64) | data formatting | bytes 1572864

commit v6 on v5

--- a/solution.py
+++ b/solution.py
@@ -95,8 +95,17 @@
                    kvs.at[d, hh, blk], kvr.at[slot, h, blk], chip, hh) for blk in range(2)]
 
     dirs = [kv_copies(0, 0), kv_copies(1, 0), kv_copies(0, 1), kv_copies(1, 1)]
-    for cp in dirs[0] + dirs[1]:
-        cp.start()
+
+    def kv_each(d, f):
+        f(dirs[d][0])
+        dst = jnp.where(h == d % 2, right, left)
+
+        @pl.when(jnp.logical_or(c > dst, jnp.logical_and(d % 2 == 0, c > opp)))
+        def _():
+            f(dirs[d][1])
+
+    for d in (0, 1):
+        kv_each(d, lambda cp: cp.start())
     project_kv(1)
     for blk in range(2):
         kvbuf[OWN, blk, pl.ds(off(blk, h), seg), :] = kv_send[h, blk * seg:(blk + 1) * seg, :]
@@ -107,6 +116,7 @@
                            kvps.at[blk], kvr.at[OWN, h, blk], c, ho))
     for cp in kv_sends:
         cp.start()
+    kv_each(2, lambda cp: cp.start())
 
     def project(dst, src, grp, w_is_q):
         for p in range(groups // 2):
@@ -140,11 +150,8 @@
     q_sends = xsends(q_send, qbuf, 0)
     for cp in q_sends:
         cp.start()
-    for cp in dirs[2]:
-        cp.start()
     project(to_own(qbuf), x_v, h, True)
-    for cp in dirs[3]:
-        cp.start()
+    kv_each(3, lambda cp: cp.start())
     ld_y.wait()
     ld_o[0].wait()
     project(to_send(do_send), dy_v, ho, False)
@@ -154,22 +161,23 @@
     ld_o[1].wait()
     project(to_own(dobuf), dy_v, h, False)
 
-    def relay(start):
-        cps = []
-        for core, slot, chip in ((0, LF, right), (1, RT, left)):
+    def relay_each(f):
+        for core, slot, src, dst in ((0, LF, left, right), (1, RT, right, left)):
             for blk in range(2):
                 view = kvbuf.at[slot, blk, pl.ds(off(blk, core), seg), :]
                 cp = rc(view, kvbuf.at[OP, blk, pl.ds(off(blk, core), seg), :],
-                        kvrs.at[core, blk], kvr.at[OP, core, blk], chip, h)
-                if start:
-                    rc(view, view, kvs.at[0, 0, blk], kvr.at[slot, core, blk], chip, h).wait_recv()
-                    cp.start()
-                cps.append(cp)
-        return cps
+                        kvrs.at[core, blk], kvr.at[OP, core, blk], dst, h)
+                wt = rc(view, view, kvs.at[0, 0, blk], kvr.at[slot, core, blk], dst, h)
+                goes = jnp.logical_or(blk == 0, src > dst)
+                f(cp, wt, jnp.logical_or(goes, src > c), goes)
+
+    def relay_start(cp, wt, came, goes):
+        pl.when(came)(lambda: wt.wait_recv())
+        pl.when(goes)(lambda: cp.start())
 
     @pl.when(h == 0)
     def _():
-        relay(True)
+        relay_each(relay_start)
 
     def fwd(ent, t, slot, blk, diag, init):
         kv = kvbuf[slot, blk]
@@ -220,7 +228,7 @@
 
     @pl.when(h == 1)
     def _():
-        relay(True)
+        relay_each(relay_start)
 
     def owner_of(slot):
         return jnp.where(slot == LF, left, jnp.where(slot == RT, right, opp))
@@ -228,21 +236,15 @@
     def fwd_body(i, carry):
         slot = i + 1
 
-        @pl.when(i == 0)
-        def _():
-            for blk in range(2):
-                wait_kv(LF, 1, blk)
-
-        @pl.when(i == 1)
-        def _():
-            for blk in range(2):
-                wait_kv(RT, 0, blk)
-
-        @pl.when(i == 2)
-        def _():
-            for core in range(2):
-                for blk in range(2):
-                    wait_kv(OP, core, blk)
+        for n, waits in enumerate((((LF, 1),), ((RT, 0),), ((OP, 0), (OP, 1)))):
+            @pl.when(i == n)
+            def _():
+                for sl, core in waits:
+                    wait_kv(sl, core, 0)
+
+                    @pl.when((left, right, opp)[n] > c)
+                    def _():
+                        wait_kv(sl, core, 1)
 
         later = (owner_of(slot) > c).astype(jnp.int32)
         fwd(3 + 2 * i, 1, slot, 0, False, False)
@@ -489,8 +491,11 @@
         else:
             out_v[...] = (acc[...] + dot(dkv[1], wkvt[1])).astype(BF)
 
-    for cp in kv_sends + sum(dirs, []) + q_sends + do_sends + relay(False) + fo_copies + [dq_copy]:
+    for cp in kv_sends + q_sends + do_sends + fo_copies + [dq_copy]:
         cp.wait_send()
+    for d in range(4):
+        kv_each(d, lambda cp: cp.wait_send())
+    relay_each(lambda cp, wt, came, goes: pl.when(goes)(lambda: cp.wait_send()))
     for blk in range(2):
         m1_each(blk, lambda cp: cp.wait_send())
     for slot in (LF, RT):

time: 36.4 us -> 36.3 us (level)
  no operation moved by 1% of the time
where the time goes in v6:
time: 36.3 us
  Pallas kernels  35.4 us (98%)
  local copies, waits for them, and re-layouts  0.88 us (2%)
    pallas_call x1, Pallas kernels, device_fn(): pl.pallas_call(functools.partial(kernel, n_dev), out_shape=pltpu.VMEM((ro...  35.4 us
    unnamed x1, local copies, waits for them, and re-layouts  0.88 us

profile of v6, /device:TPU:122, one launch (start us, length us, event | category | flops | bytes accessed | tf_op | source)
XLA Modules:
  0.0 36.3 jit_solution(14909417101740316947)
XLA Ops:
  0.0 35.4 %shard_map.64 = bf16[256,1536]{1,0:T(8,128)(2,1)S(1)} custom-call(bf16[256,1536]{1,0:T(8,128)(2,1)} %x_hbm.1, bf16[256,1536]{1,0:T(8,128)(2,1)} %dy_hbm.1, bf16[12,1536,128]{2,1,0:T(8,128)(2,1)} %bitcast.4, bf16[3072,128]{1,0:T(8,128)(2,1)} %bitcast.6, bf16[3072,128]{1,0:T(8,128)(2,1)} %bitcast.7, bf16[1536,1536]{1,0:T(8,128)(2,1)} %bitcast.5), custom_call_target="tpu_custom_call" | custom-call | tf_op jit(solution)/shard_map/pallas_call | solution.py:543
  35.4 0.9 %copy.8 = bf16[256,1536]{1,0:T(8,128)(2,1)} copy(bf16[256,1536]{1,0:T(8,128)(2,1)S(1)} %shard_map.64) | data formatting | bytes 1572864
